TPU v7x, 32 devices: a whole 2x2x4 slice. The times are simulated.
32 devices in a mesh: layer: 4 (over y, core), col: 4 (over z), row: 2 (over x).
Axes of the slice: x: 2, y: 2, z: 4, core: 2. Of those that a mesh axis runs over, the one named last changes fastest.
Arguments:
- activations: bfloat16 [4, 768, 4096], P(None, ('layer', 'row'), 'col'), may hold values from -6 to 6
- out_grads: bfloat16 [4, 768, 11008], P(None, ('layer', 'col'), 'row'), may hold values from -0.02734375 to 0.02734375
- basis_in: bfloat16 [4, 4096, 4096], P('layer', 'col', 'row'), may hold values from -0.09375 to 0.09375
- basis_out: bfloat16 [4, 11008, 11008], P('layer', 'row', 'col'), may hold values from -0.0546875 to 0.0546875
- eigenvalues: float32 [4, 11008, 4096], P('layer', 'col', 'row'), may hold values from 0.01 to 10
- damping: float32 [4], P('layer'), may hold values from 0.05 to 0.5
- layer_order: int32 [4], replicated, may hold values from 0 to 3, each once
- query_ids: int32 [256], replicated, may hold values from 0 to 3, never falling along the last dimension, each value on 1 to 128 neighbouring positions
- train_ids: int32 [512], replicated, may hold values from 0 to 15, never falling along the last dimension, each value on 1 to 64 neighbouring positions
Outputs:
- scores: float32 [4, 16], replicated
Inputs may be any that keep to these rules, and one draw needn't show every extreme that they name: `layer_order`: each slot's layer appears once. `query_ids`: never falling; every query example has 1 to 128 tokens. `train_ids`: never falling; every train example has 1 to 64 tokens.
All inputs are finite; a program needn't handle non-finite values.
Results may differ from a plain program's by a relative error of at most 0.02.
Values may be sent and summed in bfloat16 or wider, within the bound.
No kernel may reach another device: no remote copies, remote signals or barrier semaphores. Data moves between devices by JAX's collectives and lax.ppermute only.
A program may use at most 192 MiB of HBM per device.

v0:
```python
import jax
import jax.numpy as jnp
from jax import lax
from jax.sharding import PartitionSpec as P

QUERIES = 4
TRAIN = 16


def body(
    activations,
    out_grads,
    basis_in,
    basis_out,
    eigenvalues,
    damping,
    layer_order,
    query_ids,
    train_ids,
):
    slot_count = basis_in.shape[0]
    layer_groups = lax.axis_size("layer")
    row_count = lax.axis_size("row")
    col_count = lax.axis_size("col")
    ordered_in = jnp.take(activations, layer_order, axis=0)
    ordered_out = jnp.take(out_grads, layer_order, axis=0)
    in_block = ordered_in.shape[1]
    moved_in = lax.all_to_all(ordered_in, "layer", split_axis=0, concat_axis=1, tiled=True)
    shaped_in = moved_in.reshape(slot_count, layer_groups, in_block, moved_in.shape[2])
    joined_in = lax.all_gather(shaped_in, "row", axis=2, tiled=True)
    inputs_full = joined_in.reshape(
        slot_count, layer_groups * row_count * in_block, moved_in.shape[2]
    )
    out_block = ordered_out.shape[1]
    moved_out = lax.all_to_all(ordered_out, "layer", split_axis=0, concat_axis=1, tiled=True)
    shaped_out = moved_out.reshape(slot_count, layer_groups, out_block, moved_out.shape[2])
    joined_out = lax.all_gather(shaped_out, "col", axis=2, tiled=True)
    grads_full = joined_out.reshape(
        slot_count, layer_groups * col_count * out_block, moved_out.shape[2]
    )
    partial_in = jnp.einsum(
        "ltc,lcj->ltj", inputs_full, basis_in, preferred_element_type=jnp.float32
    )
    rotated_in = lax.psum(partial_in.astype(jnp.bfloat16), "col")
    partial_out = jnp.einsum(
        "ltr,lri->lti", grads_full, basis_out, preferred_element_type=jnp.float32
    )
    rotated_out = lax.psum(partial_out.astype(jnp.bfloat16), "row")
    query_tokens = query_ids.shape[0]
    query_mask = (query_ids[None, :] == jnp.arange(QUERIES, dtype=jnp.int32)[:, None]).astype(
        jnp.bfloat16
    )
    train_onehot = (train_ids[:, None] == jnp.arange(TRAIN, dtype=jnp.int32)[None, :]).astype(
        jnp.float32
    )
    query_in = rotated_in[0, :query_tokens]
    query_out = rotated_out[0, :query_tokens]
    train_in = rotated_in[0, query_tokens:]
    train_out = rotated_out[0, query_tokens:]
    masked = query_mask[:, :, None] * query_in[None, :, :]
    query_gram = jnp.einsum("si,qsj->qij", query_out, masked, preferred_element_type=jnp.float32)
    precond = (query_gram / (eigenvalues[0] + damping[0])).astype(jnp.bfloat16)
    mapped = jnp.einsum("ui,qij->quj", train_out, precond, preferred_element_type=jnp.float32)
    values = jnp.sum(mapped * train_in[None, :, :], axis=2)
    total = jnp.dot(values, train_onehot, precision=lax.Precision.HIGHEST)
    return lax.psum(total, ("layer", "col", "row"))


def solution(mesh):
    in_specs = (
        P(None, ("layer", "row"), "col"),
        P(None, ("layer", "col"), "row"),
        P("layer", "col", "row"),
        P("layer", "row", "col"),
        P("layer", "col", "row"),
        P("layer"),
        P(),
        P(),
        P(),
    )
    out_specs = P()
    return jax.shard_map(body, mesh=mesh, in_specs=in_specs, out_specs=out_specs, check_vma=False)
```

profile of v0, /device:TPU:0, one launch (start us, length us, event | category | flops | bytes accessed | tf_op | source)
XLA Modules:
  0.0 537.3 jit_solution(4422896807830578401)
XLA Ops:
  6.5 0.0 copy-start
  6.5 0.8 compare_and_fusion
  7.3 0.7 compare_select_fusion
  8.0 1.7 gather_fusion
  9.8 1.0 broadcast_select_fusion.1
  10.8 4.3 all-to-all-start
  15.0 0.0 copy-done
  15.0 2.1 gather_fusion.1
  17.1 3.2 broadcast_select_fusion
  20.3 6.3 %all-to-all-done = bf16[4,96,1024]{2,1,0:T(8,128)(2,1)S(1)} async-done(((bf16[4,96,1024]{2,1,0:T(8,128)(2,1)}), bf16[4,96,1024]{2,1,0:T(8,128)(2,1)S(1)}, u32[]{:S(2)}, u32[]{:S(2)}) %all-to-all-start) | async-done | bytes 786464 | tf_op jit(solution)/shard_map/all_to_all | solution.py:28
  26.7 0.0 copy-start.3
  26.7 3.6 all-to-all-start.1
  30.3 0.0 all-gather.5.cloned.1.call-start
  30.3 0.0 copy-done.3
  30.3 0.7 all-gather.5.cloned.1.call-update
  31.0 0.0 all-gather.7.cloned.1.call-start
  31.1 25.0 %all-to-all-done.1 = bf16[4,48,5504]{2,1,0:T(8,128)(2,1)S(1)} async-done(((bf16[4,48,5504]{2,1,0:T(8,128)(2,1)}), bf16[4,48,5504]{2,1,0:T(8,128)(2,1)S(1)}, u32[]{:S(2)}, u32[]{:S(2)}) %all-to-all-start.1) | async-done | bytes 2113568 | tf_op jit(solution)/shard_map/all_to_all | solution.py:35
  56.1 0.0 copy-start.2
  56.1 1.3 copy-done.2
  57.4 0.0 all-gather.7.cloned.1.call-update
  57.5 0.0 all-reduce.3.cloned.1.call-start
  57.5 4.7 all-gather.5.cloned.1.call-done
  62.2 7.7 %fusion.18 = bf16[1,768,2048]{2,1,0:T(8,128)(2,1)} fusion(bf16[768,1024]{1,0:T(8,128)(2,1)} %bitcast.69, bf16[1,1024,2048]{2,1,0:T(8,128)(2,1)} %param.11), kind=kOutput, calls=%fused_computation.16 | convolution fusion | flops 3222798336 | bytes 8912896 | tf_op jit(solution)/shard_map/ltc,lcj->ltj/dot_general | solution.py:41
  70.0 0.0 all-reduce.3.cloned.1.call-update
  70.0 0.2 all-reduce.5.cloned.1.call-start
  70.2 144.3 %all-gather.7.cloned.1.call-done = bf16[4,192,5504]{2,1,0:T(8,128)(2,1)} async-done(((bf16[4,48,5504]{2,1,0:T(8,128)(2,1)}), bf16[4,192,5504]{2,1,0:T(8,128)(2,1)}) %all-gather.7.cloned.1.call-update) | async-done | bytes 8454160 | tf_op jit(solution)/shard_map/all_gather | solution.py:37
  214.5 31.3 %fusion.8 = bf16[1,768,2752]{1,2,0:T(8,128)(2,1)} fusion(bf16[768,5504]{1,0:T(8,128)(2,1)} %bitcast.68, bf16[1,5504,2752]{1,2,0:T(8,128)(2,1)} %param.12), kind=kOutput, calls=%fused_computation.11 | convolution fusion | flops 23267917824 | bytes 42975232 | tf_op jit(solution)/shard_map/ltr,lri->lti/dot_general | solution.py:45
  245.8 0.0 copy-start.4
  245.8 0.0 all-reduce.5.cloned.1.call-update
  246.5 0.0 copy-done.4
  246.5 17.0 %add_bitcast_fusion = f32[2752,2048]{1,0:T(8,128)} fusion(f32[1,2752,2048]{2,1,0:T(8,128)} %param.13, f32[]{:T(128)} %bitcast.67), kind=kLoop, calls=%fused_computation.7 | loop fusion | flops 5636096 | bytes 45088772 | tf_op jit(solution)/shard_map/div | solution.py:62
  263.5 72.7 %all-reduce.3.cloned.1.call-done = bf16[1,768,2048]{2,1,0:T(8,128)(2,1)} async-done(((bf16[1,768,2048]{2,1,0:T(8,128)(2,1)}), bf16[1,768,2048]{2,1,0:T(8,128)(2,1)}) %all-reduce.3.cloned.1.call-update) | async-done | bytes 3145744 | tf_op jit(solution)/shard_map/psum | solution.py:44
  336.2 4.1 fusion.21
  340.2 5.4 %copy.12 = f32[512,2048]{0,1:T(8,128)} copy(f32[512,2048]{1,0:T(8,128)} %fusion.21) | data formatting | bytes 8388608 | tf_op jit(solution)/shard_map/mul | solution.py:64
  345.7 1.3 slice_bitcast_fusion.6
  347.0 99.2 %all-reduce.5.cloned.1.call-done = bf16[1,768,2752]{1,2,0:T(8,128)(2,1)} async-done(((bf16[1,768,2752]{1,2,0:T(8,128)(2,1)}), bf16[1,768,2752]{1,2,0:T(8,128)(2,1)}) %all-reduce.5.cloned.1.call-update) | async-done | bytes 4227088 | tf_op jit(solution)/shard_map/psum | solution.py:48
  446.1 3.6 slice_bitcast_fusion.13
  449.7 0.0 copy-start.5
  449.7 0.0 copy-start.1
  449.7 41.4 %fusion.4 = f32[4,512]{1,0:T(4,128)S(1)} fusion(f32[512,2048]{0,1:T(8,128)} %copy.12, f32[2752,2048]{1,0:T(8,128)} %add_bitcast_fusion, bf16[1,768,2752]{1,2,0:T(8,128)(2,1)} %all-reduce.5.cloned.1.call-done, bf16[256,2048]{1,0:T(8,128)(2,1)S(1)} %slice_bitcast_fusion.6, bf16[4,256]{1,0:T(4,128)(2,1)S(1)} %fusion.28, ...), kind=kOutput, calls=%fused_computation.9 | convolution fusion | flops 34690039808 | bytes 32024576 | tf_op jit(solution)/shard_map/ui,qij->quj/dot_general | solution.py:63
  491.1 0.0 copy-done.5
  491.2 0.3 fusion.26
  491.4 39.3 %psum.23 = f32[4,16]{1,0:T(4,128)} all-reduce(f32[4,16]{1,0:T(4,128)S(1)} %fusion.26), channel_id=1, replica_groups=mesh['layer'=4,'col'=4,'row'=2] {'layer','col','row'}, use_global_device_ids=true, to_apply=%region_3.4 | all-reduce | flops 64 | bytes 512 | tf_op jit(solution)/shard_map/psum | solution.py:66
  530.7 0.0 copy-done.1
  (2 shorter events, 0.0 us)
Async XLA Ops:
  6.5 8.5 %copy-start = (bf16[4,48,5504]{2,1,0:T(8,128)(2,1)S(1)}, bf16[4,48,5504]{2,1,0:T(8,128)(2,1)}, u32[]{:S(2)}) copy-start(bf16[4,48,5504]{2,1,0:T(8,128)(2,1)} %param.10) | copy-start | bytes 6340612
  10.8 15.9 %all-to-all-start = ((bf16[4,96,1024]{2,1,0:T(8,128)(2,1)}), bf16[4,96,1024]{2,1,0:T(8,128)(2,1)S(1)}, u32[]{:S(2)}, u32[]{:S(2)}) async-start(bf16[4,96,1024]{2,1,0:T(8,128)(2,1)} %broadcast_select_fusion.1), calls=%async_computation | async-start | bytes 1572864 | tf_op jit(solution)/shard_map/all_to_all | solution.py:28
  26.7 3.7 copy-start.3
  26.7 29.4 %all-to-all-start.1 = ((bf16[4,48,5504]{2,1,0:T(8,128)(2,1)}), bf16[4,48,5504]{2,1,0:T(8,128)(2,1)S(1)}, u32[]{:S(2)}, u32[]{:S(2)}) async-start(bf16[4,48,5504]{2,1,0:T(8,128)(2,1)} %broadcast_select_fusion), calls=%async_computation.1 | async-start | bytes 4227072 | tf_op jit(solution)/shard_map/all_to_all | solution.py:35
  30.3 31.9 %all-gather.5.cloned.1.call-start = ((), (), s32[]{:S(2)}) async-start(), calls=%async_computation.4 | async-start | bytes 2359296 | tf_op jit(solution)/shard_map/all_gather | solution.py:30
  31.0 183.5 %all-gather.7.cloned.1.call-start = ((), (), s32[]{:S(2)}) async-start(), calls=%async_computation.5 | async-start | bytes 10567680 | tf_op jit(solution)/shard_map/all_gather | solution.py:37
  56.1 1.3 copy-start.2
  57.5 278.7 %all-reduce.3.cloned.1.call-start = ((), (), s32[]{:S(2)}) async-start(), calls=%async_computation.2 | async-start | bytes 6291456 | tf_op jit(solution)/shard_map/psum | solution.py:44
  70.0 376.1 %all-reduce.5.cloned.1.call-start = ((), (), s32[]{:S(2)}) async-start(), calls=%async_computation.3 | async-start | bytes 8454144 | tf_op jit(solution)/shard_map/psum | solution.py:48
  245.8 0.7 copy-start.4
  449.7 41.5 %copy-start.5 = (s32[512]{0:T(512)S(1)}, s32[512]{0:T(512)}, u32[]{:S(2)}) copy-start(s32[512]{0:T(512)} %param.17) | copy-start | bytes 6148
  449.7 81.0 %copy-start.1 = (bf16[4,48,5504]{2,1,0:T(8,128)(2,1)S(1)}, bf16[4,48,5504]{2,1,0:T(8,128)(2,1)}, u32[]{:S(2)}) copy-start(bf16[4,48,5504]{2,1,0:T(8,128)(2,1)} %param.10) | copy-start | bytes 6340612
Sparse Core Ops, SparseCore 0:
  32.6 29.5 all-gather.4
  63.8 150.6 all-gather.6
  216.9 119.2 all-reduce.2
  338.5 107.6 all-reduce.4
where the time goes:
time: 538 us; the launch traced here: 537 us
  waiting for transfers between devices  353 us (66%)
  matrix products  80.7 us (15%)
  blocking collectives  39.3 us (7%)
  other arithmetic  26.7 us (5%)
  local copies, waits for them, and re-layouts  15.5 us (3%)
  between operations  13.9 us (3%)
  starting transfers between devices  8.21 us (2%)
    all_gather x1, waiting for transfers between devices, body(): joined_out = lax.all_gather(shaped_out, 'col', axis=2, tiled=True)  144 us
    psum x1, waiting for transfers between devices, body(): rotated_out = lax.psum(partial_out.astype(jnp.bfloat16), 'row')  99.2 us
    psum x1, waiting for transfers between devices, body(): rotated_in = lax.psum(partial_in.astype(jnp.bfloat16), 'col')  72.7 us
    dot_general x1, matrix products, body(): jnp.einsum('ui,qij->quj', train_out, precond, preferred_element_type=jnp....  41.4 us
    psum x1, blocking collectives, body(): return lax.psum(total, ('layer', 'col', 'row'))  39.3 us
    dot_general x1, matrix products, body(): jnp.einsum('ltr,lri->lti', grads_full, basis_out, preferred_element_type=...  31.3 us
    all_to_all x1, waiting for transfers between devices, body(): lax.all_to_all(ordered_out, 'layer', split_axis=0, concat_axis=1, tiled=T...  25 us
    div x1, other arithmetic, body(): precond = (query_gram / (eigenvalues[0] + damping[0])).astype(jnp.bfloat16)  17 us
  transfers between devices with their start and end apart: 6, of which 6 were waited for; matrix products, arithmetic and copies ran while one was open for 13% of the time, Pallas kernels for 0%

commit v1 on v0

--- a/solution.py
+++ b/solution.py
@@ -45,7 +45,7 @@
     partial_out = jnp.einsum(
         "ltr,lri->lti", grads_full, basis_out, preferred_element_type=jnp.float32
     )
-    rotated_out = lax.psum(partial_out.astype(jnp.bfloat16), "row")
+    rotated_out = jnp.sum(lax.all_gather(partial_out.astype(jnp.bfloat16), "row"), axis=0)
     query_tokens = query_ids.shape[0]
     query_mask = (query_ids[None, :] == jnp.arange(QUERIES, dtype=jnp.int32)[:, None]).astype(
         jnp.bfloat16

time: 538 us -> 579 us (1.076)
  other arithmetic: 26.7 us -> 51.8 us
  local copies, waits for them, and re-layouts: 15.5 us -> 33.4 us
    psum x1 -> x0, waiting for transfers between devices: 99.2 us -> none  [body(): rotated_out = lax.psum(partial_out.astype(jnp.bfloat16), 'row')]
    all_gather x0 -> x1, waiting for transfers between devices: none -> 96.6 us  [body(): lax.all_gather(partial_out.astype(jnp.bfloat16), 'row')]
    reduce_sum x0 -> x1, other arithmetic: none -> 25 us  [body(): jnp.sum(lax.all_gather(partial_out.astype(jnp.bfloat16), 'row'), axis=0)]
    all_gather x0 -> x1, local copies, waits for them, and re-layouts: none -> 17.7 us  [body(): lax.all_gather(partial_out.astype(jnp.bfloat16), 'row')]
where the time goes in v1:
time: 579 us; the launch traced here: 578 us
  waiting for transfers between devices  350 us (60%)
  matrix products  80.8 us (14%)
  other arithmetic  51.8 us (9%)
  blocking collectives  39.3 us (7%)
  local copies, waits for them, and re-layouts  33.4 us (6%)
  between operations  13.9 us (2%)
  starting transfers between devices  8.21 us (1%)
    all_gather x1, waiting for transfers between devices, body(): joined_out = lax.all_gather(shaped_out, 'col', axis=2, tiled=True)  144 us
    all_gather x1, waiting for transfers between devices, body(): lax.all_gather(partial_out.astype(jnp.bfloat16), 'row')  96.6 us
    psum x1, waiting for transfers between devices, body(): rotated_in = lax.psum(partial_in.astype(jnp.bfloat16), 'col')  72.7 us
    dot_general x1, matrix products, body(): jnp.einsum('ui,qij->quj', train_out, precond, preferred_element_type=jnp....  41.4 us
    psum x1, blocking collectives, body(): return lax.psum(total, ('layer', 'col', 'row'))  39.3 us
    dot_general x1, matrix products, body(): jnp.einsum('ltr,lri->lti', grads_full, basis_out, preferred_element_type=...  31.3 us
    reduce_sum x1, other arithmetic, body(): jnp.sum(lax.all_gather(partial_out.astype(jnp.bfloat16), 'row'), axis=0)  25 us
    all_to_all x1, waiting for transfers between devices, body(): lax.all_to_all(ordered_out, 'layer', split_axis=0, concat_axis=1, tiled=T...  25 us
  transfers between devices with their start and end apart: 6, of which 6 were waited for; matrix products, arithmetic and copies ran while one was open for 13% of the time, Pallas kernels for 0%

profile of v1, /device:TPU:0, one launch (start us, length us, event | category | flops | bytes accessed | tf_op | source)
XLA Modules:
  0.0 577.7 jit_solution(12751348106880920039)
XLA Ops:
  6.5 0.0 copy-start
  6.5 0.8 compare_and_fusion
  7.3 0.7 compare_select_fusion
  8.0 1.7 gather_fusion
  9.8 1.0 broadcast_select_fusion.1
  10.8 4.3 all-to-all-start
  15.0 0.0 copy-done
  15.0 2.1 gather_fusion.1
  17.1 3.2 broadcast_select_fusion
  20.3 6.3 %all-to-all-done = bf16[4,96,1024]{2,1,0:T(8,128)(2,1)S(1)} async-done(((bf16[4,96,1024]{2,1,0:T(8,128)(2,1)}), bf16[4,96,1024]{2,1,0:T(8,128)(2,1)S(1)}, u32[]{:S(2)}, u32[]{:S(2)}) %all-to-all-start) | async-done | bytes 786464 | tf_op jit(solution)/shard_map/all_to_all | solution.py:28
  26.7 0.0 copy-start.3
  26.7 3.6 all-to-all-start.1
  30.3 0.0 all-gather.7.cloned.1.call-start
  30.3 0.0 copy-done.3
  30.3 0.7 all-gather.7.cloned.1.call-update
  31.0 0.0 all-gather.9.cloned.1.call-start
  31.1 25.0 %all-to-all-done.1 = bf16[4,48,5504]{2,1,0:T(8,128)(2,1)S(1)} async-done(((bf16[4,48,5504]{2,1,0:T(8,128)(2,1)}), bf16[4,48,5504]{2,1,0:T(8,128)(2,1)S(1)}, u32[]{:S(2)}, u32[]{:S(2)}) %all-to-all-start.1) | async-done | bytes 2113568 | tf_op jit(solution)/shard_map/all_to_all | solution.py:35
  56.1 0.0 copy-start.2
  56.1 1.3 copy-done.2
  57.4 0.0 all-gather.9.cloned.1.call-update
  57.4 0.0 all-reduce.2.cloned.1.call-start
  57.5 4.7 all-gather.7.cloned.1.call-done
  62.2 7.8 %fusion.15 = bf16[1,768,2048]{2,1,0:T(8,128)(2,1)} fusion(bf16[768,1024]{1,0:T(8,128)(2,1)} %bitcast.70, bf16[1,1024,2048]{2,1,0:T(8,128)(2,1)} %param.11), kind=kOutput, calls=%fused_computation.15 | convolution fusion | flops 3222798336 | bytes 8912896 | tf_op jit(solution)/shard_map/ltc,lcj->ltj/dot_general | solution.py:41
  70.0 0.0 all-reduce.2.cloned.1.call-update
  70.0 0.2 all-gather.11.cloned.1.call-start
  70.3 144.3 %all-gather.9.cloned.1.call-done = bf16[4,192,5504]{2,1,0:T(8,128)(2,1)} async-done(((bf16[4,48,5504]{2,1,0:T(8,128)(2,1)}), bf16[4,192,5504]{2,1,0:T(8,128)(2,1)}) %all-gather.9.cloned.1.call-update) | async-done | bytes 8454160 | tf_op jit(solution)/shard_map/all_gather | solution.py:37
  214.5 31.3 %fusion.5 = bf16[768,2752]{0,1:T(8,128)(2,1)} fusion(bf16[768,5504]{1,0:T(8,128)(2,1)} %bitcast.69, bf16[1,5504,2752]{1,2,0:T(8,128)(2,1)} %param.12), kind=kOutput, calls=%fused_computation.10 | convolution fusion | flops 23267917824 | bytes 42975232 | tf_op jit(solution)/shard_map/ltr,lri->lti/dot_general | solution.py:45
  245.8 0.0 copy-start.4
  245.8 0.0 all-gather.11.cloned.1.call-update
  246.5 0.0 copy-done.4
  246.5 17.0 %add_bitcast_fusion = f32[2752,2048]{1,0:T(8,128)} fusion(f32[1,2752,2048]{2,1,0:T(8,128)} %param.13, f32[]{:T(128)} %bitcast.66), kind=kLoop, calls=%fused_computation.7 | loop fusion | flops 5636096 | bytes 45088772 | tf_op jit(solution)/shard_map/div | solution.py:62
  263.5 72.7 %all-reduce.2.cloned.1.call-done = bf16[1,768,2048]{2,1,0:T(8,128)(2,1)} async-done(((bf16[1,768,2048]{2,1,0:T(8,128)(2,1)}), bf16[1,768,2048]{2,1,0:T(8,128)(2,1)}) %all-reduce.2.cloned.1.call-update) | async-done | bytes 3145744 | tf_op jit(solution)/shard_map/psum | solution.py:44
  336.2 4.1 fusion.18
  340.2 5.4 copy.14
  345.7 1.5 slice_bitcast_fusion.6
  347.2 96.6 %all-gather.11.cloned.1.call-done = bf16[1536,2752]{0,1:T(8,128)(2,1)} async-done(((bf16[768,2752]{0,1:T(8,128)(2,1)}), bf16[1536,2752]{0,1:T(8,128)(2,1)}) %all-gather.11.cloned.1.call-update) | async-done | bytes 8454160 | tf_op jit(solution)/shard_map/all_gather | solution.py:48
  443.8 17.7 %reshape.86 = bf16[2,768,2752]{1,0,2:T(2,128)(2,1)} reshape(bf16[1536,2752]{0,1:T(8,128)(2,1)} %all-gather.11.cloned.1.call-done) | data formatting | bytes 16908288 | tf_op jit(solution)/shard_map/all_gather | solution.py:48
  461.6 25.0 %reduce.2 = bf16[768,2752]{0,1:T(8,128)(2,1)} reduce(bf16[2,768,2752]{1,0,2:T(2,128)(2,1)} %reshape.86, bf16[]{:T(256)} %constant.30.clone.1), dimensions={0}, to_apply=%region_1.2 | reduce | flops 2113536 | bytes 12681218 | tf_op jit(solution)/shard_map/reduce_sum | solution.py:48
  486.6 3.6 slice_bitcast_fusion.13
  490.1 0.0 copy-start.5
  490.1 0.0 copy-start.1
  490.1 41.4 %fusion.4 = f32[4,512]{1,0:T(4,128)S(1)} fusion(f32[512,2048]{0,1:T(8,128)} %copy.14, f32[2752,2048]{1,0:T(8,128)} %add_bitcast_fusion, bf16[1,768,2752]{1,2,0:T(8,128)(2,1)} %bitcast.68, bf16[256,2048]{1,0:T(8,128)(2,1)S(1)} %slice_bitcast_fusion.6, bf16[4,256]{1,0:T(4,128)(2,1)S(1)} %fusion.25, bf16[512,2752,1]{0,1,2:T(8,128)(2,1)} %slice_bitcast_fusion.13), kind=kOutput, calls=%fused_computation.9 | convolution fusion | flops 34690039808 | bytes 32024576 | tf_op jit(solution)/shard_map/ui,qij->quj/dot_general | solution.py:63
  531.6 0.0 copy-done.5
  531.6 0.3 fusion.23
  531.9 39.3 %psum.15 = f32[4,16]{1,0:T(4,128)} all-reduce(f32[4,16]{1,0:T(4,128)S(1)} %fusion.23), channel_id=1, replica_groups=mesh['layer'=4,'col'=4,'row'=2] {'layer','col','row'}, use_global_device_ids=true, to_apply=%region_3.4 | all-reduce | flops 64 | bytes 512 | tf_op jit(solution)/shard_map/psum | solution.py:66
  571.2 0.0 copy-done.1
  (2 shorter events, 0.0 us)
Async XLA Ops:
  6.5 8.5 %copy-start = (bf16[4,48,5504]{2,1,0:T(8,128)(2,1)S(1)}, bf16[4,48,5504]{2,1,0:T(8,128)(2,1)}, u32[]{:S(2)}) copy-start(bf16[4,48,5504]{2,1,0:T(8,128)(2,1)} %param.10) | copy-start | bytes 6340612
  10.8 15.9 %all-to-all-start = ((bf16[4,96,1024]{2,1,0:T(8,128)(2,1)}), bf16[4,96,1024]{2,1,0:T(8,128)(2,1)S(1)}, u32[]{:S(2)}, u32[]{:S(2)}) async-start(bf16[4,96,1024]{2,1,0:T(8,128)(2,1)} %broadcast_select_fusion.1), calls=%async_computation | async-start | bytes 1572864 | tf_op jit(solution)/shard_map/all_to_all | solution.py:28
  26.7 3.7 copy-start.3
  26.7 29.4 %all-to-all-start.1 = ((bf16[4,48,5504]{2,1,0:T(8,128)(2,1)}), bf16[4,48,5504]{2,1,0:T(8,128)(2,1)S(1)}, u32[]{:S(2)}, u32[]{:S(2)}) async-start(bf16[4,48,5504]{2,1,0:T(8,128)(2,1)} %broadcast_select_fusion), calls=%async_computation.1 | async-start | bytes 4227072 | tf_op jit(solution)/shard_map/all_to_all | solution.py:35
  30.3 31.9 %all-gather.7.cloned.1.call-start = ((), (), s32[]{:S(2)}) async-start(), calls=%async_computation.3 | async-start | bytes 2359296 | tf_op jit(solution)/shard_map/all_gather | solution.py:30
  31.0 183.5 %all-gather.9.cloned.1.call-start = ((), (), s32[]{:S(2)}) async-start(), calls=%async_computation.4 | async-start | bytes 10567680 | tf_op jit(solution)/shard_map/all_gather | solution.py:37
  56.1 1.3 copy-start.2
  57.4 278.7 %all-reduce.2.cloned.1.call-start = ((), (), s32[]{:S(2)}) async-start(), calls=%async_computation.2 | async-start | bytes 6291456 | tf_op jit(solution)/shard_map/psum | solution.py:44
  70.0 373.8 %all-gather.11.cloned.1.call-start = ((), (), s32[]{:S(2)}) async-start(), calls=%async_computation.5 | async-start | bytes 12681216 | tf_op jit(solution)/shard_map/all_gather | solution.py:48
  245.8 0.7 copy-start.4
  490.1 41.5 %copy-start.5 = (s32[512]{0:T(512)S(1)}, s32[512]{0:T(512)}, u32[]{:S(2)}) copy-start(s32[512]{0:T(512)} %param.17) | copy-start | bytes 6148
  490.1 81.0 %copy-start.1 = (bf16[4,48,5504]{2,1,0:T(8,128)(2,1)S(1)}, bf16[4,48,5504]{2,1,0:T(8,128)(2,1)}, u32[]{:S(2)}) copy-start(bf16[4,48,5504]{2,1,0:T(8,128)(2,1)} %param.10) | copy-start | bytes 6340612
Sparse Core Ops, SparseCore 0:
  32.6 29.5 all-gather.6
  63.8 150.6 all-gather.8
  216.9 119.2 all-reduce.1
  337.6 106.1 all-gather.10
